TPU v7x, 32 devices: a whole 2x2x4 slice. The times are simulated.
32 devices in a mesh: dp: 8 (over y, x, core), mp: 4 (over z).
Axes of the slice: x: 2, y: 2, z: 4, core: 2. Of those that a mesh axis runs over, the one named last changes fastest.
Arguments:
- tokens: bfloat16 [1024, 8192], P(('dp', 'mp')), parts along dimension 0, may hold values from -6 to 6
- norm_gain: float32 [8192], replicated, may hold values from 0.5 to 1.5
- qkv_weight: bfloat16 [8192, 10240], P(None, 'mp'), may hold values from -0.0625 to 0.0625
- qkv_bias: float32 [10240], P('mp'), may hold values from -3 to 3
- qkv_grad: bfloat16 [1024, 10240], P('dp', 'mp'), parts along dimension 0, may hold values from -6 to 6
Outputs:
- qkv: bfloat16 [1024, 10240], P('dp', 'mp'), parts along dimension 0
- tokens_grad: float32 [1024, 8192], P(('dp', 'mp')), parts along dimension 0
- gain_grad: float32 [65536], P('dp'), parts along dimension 0
- bias_grad: float32 [81920], P(('dp', 'mp')), parts along dimension 0
There are 8 independent parts, one for each index of `dp`. A program takes and returns all parts, laid end to end along the dimension named above; an argument that names none is the same for every part. Nothing has to cross between parts.
All inputs are finite; a program needn't handle non-finite values.
Results may differ from a plain program's by a relative error of at most 0.0046.
Values may be sent and summed in bfloat16 or wider, within the bound.
A program may use at most 128 MiB of HBM per device.

v0:
```python
import functools

import jax
import jax.numpy as jnp
import numpy as np
from jax import lax
from jax.experimental import pallas as pl
from jax.experimental.pallas import tpu as pltpu
from jax.sharding import PartitionSpec as P

HEAD_DIM = 128
SEQ_LEN = 32768
GROUP = 10
CHUNKS = 4
TILE_K = 512
MESH = pl.DeviceIdType.MESH


def rope_tables(rows, tok_dev, stride):
    half = HEAD_DIM // 2
    row = np.arange(rows)
    place = (row // tok_dev * stride + row % tok_dev).astype(np.float32)
    inverse = np.exp(
        -np.log(np.float32(1000000.0))
        * (np.float32(2.0) * np.arange(half).astype(np.float32) / np.float32(HEAD_DIM))
    ).astype(np.float32)
    angle = (place[:, None] * inverse[None, :]).astype(np.float32)
    cosine, sine = np.cos(angle).astype(np.float32), np.sin(angle).astype(np.float32)
    return np.concatenate([cosine, cosine], 1), np.concatenate([-sine, sine], 1)


def kernel(
    n,
    tok_h, gain_h, w_h, bias_h, grad_h, cos_h, sin_h,
    qkv, tg, gg_ref, bg_ref,
    tok, gain, w, bias, grad, cos, sin,
    low, part, held, run, acc, ng, scale_ref, gmine, gsend, grecv,
    in_sem, w_sem, send_sem, recv_sem, gsend_sem, grecv_sem,
):
    me = lax.axis_index("mp")
    rows, depth = tok.shape
    width = w.shape[1]
    heads = width // HEAD_DIM
    span = depth // CHUNKS
    tiles = depth // TILE_K
    per = tiles // CHUNKS
    f32 = jnp.float32

    has_right, has_left = me < n - 1, me > 0
    barrier = pltpu.get_barrier_semaphore()
    for there, k in ((has_right, 1), (has_left, n - 1)):
        @pl.when(there)
        def _():
            pl.semaphore_signal(
                barrier, inc=1, device_id={"mp": lax.rem(me + k, n)}, device_id_type=MESH
            )

    loads = []
    for i, (src, dst) in enumerate(
        ((tok_h, tok), (gain_h, gain.at[0]), (grad_h, grad), (cos_h, cos), (sin_h, sin), (bias_h, bias.at[0]))
    ):
        c = pltpu.make_async_copy(src, dst, in_sem.at[i])
        c.start()
        loads.append(c)

    def w_copy(i):
        k = pl.ds(pl.multiple_of(i * TILE_K, TILE_K), TILE_K)
        return pltpu.make_async_copy(w_h.at[k, :], w.at[k, :], w_sem.at[i])

    def block(s):
        return pl.ds(pl.multiple_of(s * rows, rows), rows)

    def cols(c):
        return pl.ds(pl.multiple_of(c * span, span), span)

    loads[0].wait()
    loads[1].wait()
    total = jnp.zeros((rows, 1), f32)
    for c in range(CHUNKS):
        v = tok[:, c * span:(c + 1) * span].astype(f32)
        total = total + jnp.sum(v * v, axis=1, keepdims=True)
    scale = lax.rsqrt(total / depth + 1e-06)
    scale_ref[...] = jnp.broadcast_to(scale, scale_ref.shape)
    for c in range(CHUNKS):
        ks = slice(c * span, (c + 1) * span)
        held[block(me), ks] = (tok[:, ks].astype(f32) * scale * gain[:, ks]).astype(jnp.bfloat16)
    inside = has_right & has_left

    @pl.when(inside)
    def _():
        pl.semaphore_wait(barrier, 2)

    @pl.when(jnp.logical_not(inside))
    def _():
        pl.semaphore_wait(barrier, 1)


    def transfer(way, buf, at, j, c):
        ref = buf.at[block(at), cols(c)]
        return pltpu.make_async_remote_copy(
            src_ref=ref,
            dst_ref=ref,
            send_sem=send_sem.at[way, j, c],
            recv_sem=recv_sem.at[way, j, c],
            device_id={"mp": lax.rem(me + (1 if way == 0 else n - 1), n)},
            device_id_type=MESH,
        )

    def arrive(j, c):
        for way, comes in ((0, has_left), (1, has_right)):
            @pl.when(comes)
            def _():
                transfer(way, held, 0, j - 1, c).wait_recv()

    def depart(j, c):
        for way, goes, comes, back in ((0, has_right, has_left, me), (1, has_left, has_right, n - 1 - me)):
            @pl.when(goes)
            def _():
                @pl.when(j <= back)
                def _():
                    transfer(way, held, me - j if way == 0 else me + j, j, c).start()

                @pl.when(j > back)
                def _():
                    t = n - j + me if way == 0 else j - n + me
                    slot = t + 1 if way == 0 else t

                    @pl.when(comes)
                    def _():
                        value = part[block(t), cols(c)] + run[block(slot), cols(c)].astype(f32)
                        run[block(slot), cols(c)] = value.astype(jnp.bfloat16)

                    @pl.when(jnp.logical_not(comes))
                    def _():
                        run[block(slot), cols(c)] = part[block(t), cols(c)].astype(jnp.bfloat16)

                    transfer(way, run, slot, j, c).start()

    def step(j, c):
        arrive(j, c)
        depart(j, c)

    for c in range(CHUNKS):
        for way, goes in ((0, has_right), (1, has_left)):
            @pl.when(goes)
            def _():
                transfer(way, held, me, 0, c).start()

    @pl.loop(0, tiles)
    def _(i):
        w_copy(i).start()

    for l in loads[2:]:
        l.wait()
    for h in range(heads):
        hs = slice(h * HEAD_DIM, (h + 1) * HEAD_DIM)
        x = grad[:, hs].astype(f32)
        turned = x * cos[...] - pltpu.roll(x, HEAD_DIM // 2, 1) * sin[...]
        plain = lax.rem(me * heads + h, GROUP) == GROUP - 1
        x = jnp.where(plain, x, turned)
        bg_ref[:, hs] = jnp.sum(x, axis=0, keepdims=True)
        low[:, hs] = x.astype(jnp.bfloat16)

    def backward(c):
        @pl.loop(0, per)
        def _(i):
            at = c * per + i
            w_copy(at).wait()
            k = pl.ds(pl.multiple_of(at * TILE_K, TILE_K), TILE_K)
            part[:, k] = lax.dot_general(
                low[...], w[k, :], (((1,), (1,)), ((), ())), preferred_element_type=f32
            )

    @pl.loop(0, CHUNKS)
    def _(c):
        backward(c)

        @pl.when(c > 0)
        def _():
            step(1, c - 1)

    step(1, CHUNKS - 1)

    @pl.loop(2, n - 1)
    def _(j):
        @pl.loop(0, CHUNKS)
        def _(c):
            step(j, c)

    tile_n = 640 if width % 640 == 0 else HEAD_DIM
    tiles_n = width // tile_n

    def gain_copy(k):
        return pltpu.make_async_remote_copy(
            src_ref=gsend,
            dst_ref=grecv.at[k - 1],
            send_sem=gsend_sem.at[k - 1],
            recv_sem=grecv_sem.at[k - 1],
            device_id={"mp": lax.rem(me + k, n)},
            device_id_type=MESH,
        )

    piece = span // 16

    @pl.loop(0, CHUNKS)
    def _(c):
        arrive(n - 1, c)
        for i in range(16):
            ks = pl.ds(pl.multiple_of(c * span + i * piece, piece), piece)
            share = jnp.sum(part[:, ks] * held[:, ks].astype(f32), axis=0, keepdims=True)
            gmine[c, i:i + 1, :] = share / gain[:, ks]
        gsend[c] = gmine[c].astype(jnp.bfloat16)

        @pl.when(c == CHUNKS - 1)
        def _():
            for k in range(1, n):
                gain_copy(k).start()

        depart(n - 1, c)

        @pl.loop(0, tiles_n)
        def _(i):
            ns = pl.ds(pl.multiple_of(i * tile_n, tile_n), tile_n)
            value = jnp.dot(held[:, cols(c)], w[cols(c), ns], preferred_element_type=f32)

            @pl.when(c == 0)
            def _():
                acc[:, ns] = value

            @pl.when(c > 0)
            def _():
                acc[:, ns] += value

    for h in range(heads):
        hs = slice(h * HEAD_DIM, (h + 1) * HEAD_DIM)
        x = acc[:, hs] + bias[:, hs]
        turned = x * cos[...] + pltpu.roll(x, HEAD_DIM // 2, 1) * sin[...]
        plain = lax.rem(me * heads + h, GROUP) == GROUP - 1
        qkv[:, hs] = jnp.where(plain, x, turned).astype(jnp.bfloat16)

    scale = scale_ref[:, :1]
    inner = jnp.zeros((rows, 1), f32)
    for c in range(CHUNKS):
        ks = slice(c * span, (c + 1) * span)
        if c == CHUNKS - 1:
            for k in range(1, n):
                gain_copy(k).wait_recv()
            for g in range(CHUNKS):
                total = gmine[g]
                for k in range(1, n):
                    total = total + grecv[k - 1, g].astype(f32)
                for i in range(16):
                    at = g * span + i * piece
                    gg_ref[:, at:at + piece] = total[i:i + 1, :]
        ng[:, ks] = part[block(me), ks]
        for way, comes, slot in ((0, has_left, me + 1), (1, has_right, me)):
            @pl.when(comes)
            def _():
                transfer(way, run, slot, n - 1, c).wait_recv()
                ng[:, ks] += run[block(slot), ks].astype(f32)

        product = ng[:, ks] * tok[:, ks].astype(f32)
        inner = inner + jnp.sum(product * gain[:, ks], axis=1, keepdims=True)
        tg[:, ks] = scale * gain[:, ks] * ng[:, ks]

    weight = scale * scale * scale * (inner / depth)
    for c in range(CHUNKS):
        ks = slice(c * span, (c + 1) * span)
        tg[:, ks] -= tok[:, ks].astype(f32) * weight

    @pl.loop(0, n)
    def _(j):
        @pl.loop(0, CHUNKS)
        def _(c):
            for way, goes in ((0, has_right), (1, has_left)):
                @pl.when(goes)
                def _():
                    transfer(way, held, 0, j, c).wait_send()

    for k in range(1, n):
        gain_copy(k).wait_send()


def finish(qkv, tg, gg, bg, qkv_h, tg_h, gg_h, bg_h, sem):
    moves = ((qkv, qkv_h), (tg, tg_h), (gg.at[0], gg_h), (bg.at[0], bg_h))
    copies = [pltpu.make_async_copy(src, dst, sem.at[i]) for i, (src, dst) in enumerate(moves)]
    for c in copies:
        c.start()
    for c in copies:
        c.wait()


def shards(n, tokens, norm_gain, qkv_weight, qkv_bias, qkv_grad):
    rows, depth = tokens.shape
    every, width = qkv_grad.shape
    cosine, sine = rope_tables(every, rows, SEQ_LEN // n)
    bf16, f32 = jnp.bfloat16, jnp.float32
    span = depth // CHUNKS
    dma = pltpu.SemaphoreType.DMA
    hbm = pl.BlockSpec(memory_space=pl.ANY)
    vmem = pl.BlockSpec(memory_space=pltpu.VMEM)
    results = pl.pallas_call(
        functools.partial(kernel, n),
        out_shape=(
            pltpu.VMEM((every, width), bf16),
            pltpu.VMEM((rows, depth), f32),
            pltpu.VMEM((1, depth), f32),
            pltpu.VMEM((1, width), f32),
        ),
        in_specs=[hbm] * 7,
        out_specs=[vmem] * 4,
        scratch_shapes=[
            pltpu.VMEM((rows, depth), bf16),
            pltpu.VMEM((1, depth), f32),
            pltpu.VMEM((depth, width), bf16),
            pltpu.VMEM((1, width), f32),
            pltpu.VMEM((every, width), bf16),
            pltpu.VMEM((every, HEAD_DIM), f32),
            pltpu.VMEM((every, HEAD_DIM), f32),
            pltpu.VMEM((every, width), bf16),
            pltpu.VMEM((every, depth), f32),
            pltpu.VMEM((every, depth), bf16),
            pltpu.VMEM((every + rows, depth), bf16),
            pltpu.VMEM((every, width), f32),
            pltpu.VMEM((rows, depth), f32),
            pltpu.VMEM((rows, HEAD_DIM), f32),
            pltpu.VMEM((CHUNKS, 16, span // 16), f32),
            pltpu.VMEM((CHUNKS, 16, span // 16), bf16),
            pltpu.VMEM((n - 1, CHUNKS, 16, span // 16), bf16),
            dma((6,)),
            dma((depth // TILE_K,)),
            dma((2, n, CHUNKS)),
            dma((2, n, CHUNKS)),
            dma((n - 1,)),
            dma((n - 1,)),
        ],
        compiler_params=pltpu.CompilerParams(
            collective_id=0, has_side_effects=True, vmem_limit_bytes=60000000
        ),
        cost_estimate=pl.CostEstimate(
            flops=4 * every * depth * width, bytes_accessed=2 * depth * width, transcendentals=0
        ),
    )(
        tokens, norm_gain, qkv_weight, qkv_bias, qkv_grad,
        jnp.asarray(cosine), jnp.asarray(sine),
    )
    return pl.pallas_call(
        finish,
        out_shape=(
            jax.ShapeDtypeStruct((every, width), bf16),
            jax.ShapeDtypeStruct((rows, depth), f32),
            jax.ShapeDtypeStruct((depth,), f32),
            jax.ShapeDtypeStruct((width,), f32),
        ),
        in_specs=[vmem] * 4,
        out_specs=[hbm] * 4,
        scratch_shapes=[dma((4,))],
        compiler_params=pltpu.CompilerParams(vmem_limit_bytes=1 << 20),
    )(*results)


def solution(mesh):
    in_specs = (P(("dp", "mp"), None), P(), P(None, "mp"), P("mp"), P("dp", "mp"))
    out_specs = (P("dp", "mp"), P(("dp", "mp"), None), P("dp"), P(("dp", "mp")))
    body = functools.partial(shards, mesh.shape["mp"])
    return jax.shard_map(body, mesh=mesh, in_specs=in_specs, out_specs=out_specs, check_vma=False)
```

profile of v0, /device:TPU:0, one launch (start us, length us, event | category | flops | bytes accessed | tf_op | source)
XLA Modules:
  0.0 54.8 jit_solution(11937480749961207466)
XLA Ops:
  0.6 52.9 %shard_map.102 = (bf16[128,2560]{1,0:T(8,128)(2,1)S(1)}, f32[32,8192]{1,0:T(8,128)S(1)}, f32[1,8192]{1,0:T(1,128)S(1)}, f32[1,2560]{1,0:T(1,128)S(1)}) custom-call(bf16[32,8192]{1,0:T(8,128)(2,1)} %tok_h.1, f32[8192]{0:T(1024)} %gain_h.1, bf16[8192,2560]{1,0:T(8,128)(2,1)} %w_h.1, f32[2560]{0:T(1024)} %bias_h.1, bf16[128,2560]{1,0:T(8,128)(2,1)} %grad_h.1, ...), custom_call_target="tpu_custom_call" | custom-call | flops 10737418240 | bytes 41943040 | tf_op jit(solution)/shard_map/pallas_call | solution.py:302
  53.5 1.2 %shard_map.103 = (bf16[128,2560]{1,0:T(8,128)(2,1)}, f32[32,8192]{1,0:T(8,128)}, f32[8192]{0:T(1024)}, f32[2560]{0:T(1024)}) custom-call(bf16[128,2560]{1,0:T(8,128)(2,1)S(1)} %get-tuple-element.8.qkv, f32[32,8192]{1,0:T(8,128)S(1)} %get-tuple-element.9.tg, f32[1,8192]{1,0:T(1,128)S(1)} %get-tuple-element.10.gg, f32[1,2560]{1,0:T(1,128)S(1)} %get-tuple-element.11.bg), custom_call_target="tpu_custom_call" | custom-call | tf_op jit(solution)/shard_map/pallas_call | solution.py:347
where the time goes:
time: 54.9 us; the launch traced here: 54.8 us
  Pallas kernels  54.1 us (99%)
  between operations  0.64 us (1%)
    pallas_call x1, Pallas kernels, shards(): pl.pallas_call(functools.partial(kernel, n), out_shape=(pltpu.VMEM((every...  52.9 us
    pallas_call x1, Pallas kernels, shards(): pl.pallas_call(finish, out_shape=(jax.ShapeDtypeStruct((every, width), bf...  1.23 us

commit v1 on v0

v1 whole, which is shorter than its diff:
```python
import functools

import jax
import jax.numpy as jnp
import numpy as np
from jax import lax
from jax.experimental import pallas as pl
from jax.experimental.pallas import tpu as pltpu
from jax.sharding import PartitionSpec as P

HEAD_DIM = 128
SEQ_LEN = 32768
GROUP = 10
CHUNKS = 4
TILE_K = 512
PIECES = 4
MESH = pl.DeviceIdType.MESH


def rope_tables(rows, tok_dev, stride):
    half = HEAD_DIM // 2
    row = np.arange(rows)
    place = (row // tok_dev * stride + row % tok_dev).astype(np.float32)
    inverse = np.exp(
        -np.log(np.float32(1000000.0))
        * (np.float32(2.0) * np.arange(half).astype(np.float32) / np.float32(HEAD_DIM))
    ).astype(np.float32)
    angle = (place[:, None] * inverse[None, :]).astype(np.float32)
    cosine, sine = np.cos(angle).astype(np.float32), np.sin(angle).astype(np.float32)
    return np.concatenate([cosine, cosine], 1), np.concatenate([-sine, sine], 1)


def kernel(
    n,
    tok_h, gain_h, w_h, bias_h, grad_h, cos_h, sin_h,
    qkv, tgp, tok, weight, gg_ref, bg_ref,
    raw, gain, w, bias, grad, cos, sin,
    low, part, held, run, acc, square, scale_ref, gsum, gmine, gout, gin,
    tok_sem, in_sem, w_sem, send_sem, recv_sem, gsend_sem, grecv_sem, ready,
):
    me = lax.axis_index("mp")
    rows, depth = tok.shape
    width = w.shape[1]
    heads = width // HEAD_DIM
    span = depth // CHUNKS
    tiles = depth // TILE_K
    per = tiles // CHUNKS
    half = n // 2
    f32, bf16 = jnp.float32, jnp.bfloat16

    has_right, has_left = me < n - 1, me > 0
    ways = ((0, has_right, has_left), (1, has_left, has_right))
    barrier = pltpu.get_barrier_semaphore()

    def peer(way):
        return {"mp": lax.rem(me + (1 if way == 0 else n - 1), n)}

    @pl.when(has_right)
    def _():
        pl.semaphore_signal(barrier, inc=1, device_id=peer(0), device_id_type=MESH)

    def block(s):
        return pl.ds(pl.multiple_of(s * rows, rows), rows)

    def cols(c):
        return pl.ds(pl.multiple_of(c * span, span), span)

    def tok_copy(c):
        return pltpu.make_async_copy(
            tok_h.at[:, cols(c)], raw.at[block(me), cols(c)], tok_sem.at[c]
        )

    for c in range(CHUNKS):
        tok_copy(c).start()
    loads = []
    for i, (src, dst) in enumerate(
        ((gain_h, gain.at[0]), (grad_h, grad), (cos_h, cos), (sin_h, sin), (bias_h, bias.at[0]), (tok_h, tok))
    ):
        loads.append(pltpu.make_async_copy(src, dst, in_sem.at[i]))
        loads[i].start()

    def w_copy(i):
        k = pl.ds(pl.multiple_of(i * TILE_K, TILE_K), TILE_K)
        return pltpu.make_async_copy(w_h.at[k, :], w.at[k, :], w_sem.at[i])

    def transfer(way, buf, at, j, c):
        ref = buf.at[block(at), cols(c)]
        return pltpu.make_async_remote_copy(
            src_ref=ref,
            dst_ref=ref,
            send_sem=send_sem.at[way, j, c],
            recv_sem=recv_sem.at[way, j, c],
            device_id=peer(way),
            device_id_type=MESH,
        )

    def absorb(b, c):
        v = raw[block(b), cols(c)].astype(f32)
        held[block(b), cols(c)] = (v * gain[:, cols(c)]).astype(bf16)
        v = v * v
        while v.shape[1] > HEAD_DIM:
            m = v.shape[1] // 2
            v = v[:, :m] + v[:, m:]
        if isinstance(c, int):
            old = jnp.zeros_like(v) if c == 0 else square[block(b), :]
        else:
            old = jnp.where(c == 0, jnp.zeros_like(v), square[block(b), :])
        square[block(b), :] = old + v

    def settle(b):
        total = jnp.sum(square[block(b), :], axis=1, keepdims=True)
        scale_ref[block(b), :] = jnp.broadcast_to(lax.rsqrt(total / depth + 1e-06), (rows, HEAD_DIM))

    @pl.when(has_left)
    def _():
        pl.semaphore_wait(barrier, 1)
        pl.semaphore_signal(ready, inc=1, device_id=peer(1), device_id_type=MESH)

    for c in range(CHUNKS):
        tok_copy(c).wait()

        @pl.when(has_left)
        def _():
            transfer(1, raw, me, 0, c).start()

    @pl.loop(0, tiles)
    def _(i):
        w_copy(i).start()

    @pl.when(has_right)
    def _():
        pl.semaphore_wait(ready, 1)
        for c in range(CHUNKS):
            transfer(0, raw, me, 0, c).start()

    def arrive(j, c):
        for way, goes, comes in ways:
            @pl.when(comes)
            def _():
                transfer(way, raw, 0, j - 1, c).wait_recv()

    def prepare(j, c):
        for way, goes, comes in ways:
            back = me if way == 0 else n - 1 - me

            @pl.when(goes & (j > back))
            def _():
                t = n - j + me if way == 0 else j - n + me
                slot = t + 1 if way == 0 else t

                @pl.when(comes)
                def _():
                    value = part[block(t), cols(c)] + run[block(slot), cols(c)].astype(f32)
                    run[block(slot), cols(c)] = value.astype(bf16)

                @pl.when(jnp.logical_not(comes))
                def _():
                    run[block(slot), cols(c)] = part[block(t), cols(c)].astype(bf16)

    def launch(j, c):
        for way, goes, comes in ways:
            back = me if way == 0 else n - 1 - me

            @pl.when(goes & (j <= back))
            def _():
                transfer(way, raw, me - j if way == 0 else me + j, j, c).start()

            @pl.when(goes & (j > back))
            def _():
                t = n - j + me if way == 0 else j - n + me
                transfer(way, run, t + 1 if way == 0 else t, j, c).start()

    def take(j, c):
        for way, goes, comes in ways:
            back = me if way == 0 else n - 1 - me

            @pl.when(comes & (j <= back))
            def _():
                b = me - j if way == 0 else me + j
                absorb(b, c)
                if isinstance(c, int):
                    if c == CHUNKS - 1:
                        settle(b)
                else:
                    @pl.when(c == CHUNKS - 1)
                    def _():
                        settle(b)

    def step(j, c):
        arrive(j, c)
        prepare(j, c)
        launch(j, c)
        take(j, c)

    for l in loads[:5]:
        l.wait()
    for h in range(heads):
        hs = slice(h * HEAD_DIM, (h + 1) * HEAD_DIM)
        x = grad[:, hs].astype(f32)
        turned = x * cos[...] - pltpu.roll(x, HEAD_DIM // 2, 1) * sin[...]
        plain = lax.rem(me * heads + h, GROUP) == GROUP - 1
        x = jnp.where(plain, x, turned)
        bg_ref[:, hs] = jnp.sum(x, axis=0, keepdims=True)
        low[:, hs] = x.astype(bf16)

    def backward(c):
        @pl.loop(0, per)
        def _(i):
            at = c * per + i
            w_copy(at).wait()
            k = pl.ds(pl.multiple_of(at * TILE_K, TILE_K), TILE_K)
            part[:, k] = lax.dot_general(
                low[...], w[k, :], (((1,), (1,)), ((), ())), preferred_element_type=f32
            )

    @pl.loop(0, CHUNKS)
    def _(c):
        backward(c)
        absorb(me, c)

        @pl.when(c > 0)
        def _():
            step(1, c - 1)

    settle(me)
    step(1, CHUNKS - 1)

    @pl.loop(2, half)
    def _(j):
        @pl.loop(0, CHUNKS)
        def _(c):
            step(j, c)

    for c in range(CHUNKS - 1):
        step(half, c)
    arrive(half, CHUNKS - 1)
    prepare(half, CHUNKS - 1)
    take(half, CHUNKS - 1)

    def gain_add(t, slot):
        source = part if slot is None else run
        at = slice(t * rows, (t + 1) * rows) if slot is None else slice(slot * rows, (slot + 1) * rows)
        scale = scale_ref[t * rows:(t + 1) * rows, :]

        @pl.loop(0, depth // 1024)
        def _(i):
            for p in range(1024 // HEAD_DIM):
                k = pl.ds(pl.multiple_of(i * 1024 + p * HEAD_DIM, HEAD_DIM), HEAD_DIM)
                x = source[at, k].astype(f32) * raw[t * rows:(t + 1) * rows, k].astype(f32) * scale
                total = x[:8]
                for r in range(8, rows, 8):
                    total = total + x[r:r + 8]
                gsum[:, k] += total

    gsum[...] = jnp.zeros_like(gsum)
    for t in range(n):
        @pl.when((me - t < half) & (t - me < half))
        def _():
            gain_add(t, None)

        if t + half < n:
            @pl.when(me == t + half)
            def _():
                gain_add(t, t)
        if t - half >= 0:
            @pl.when(me == t - half)
            def _():
                gain_add(t, t + 1)
    piece = depth // 16
    for i in range(16):
        gmine[i:i + 1, :] = jnp.sum(gsum[:, i * piece:(i + 1) * piece], axis=0, keepdims=True)

    def gain_copy(way):
        return pltpu.make_async_remote_copy(
            src_ref=gout.at[way],
            dst_ref=gin.at[way],
            send_sem=gsend_sem.at[way],
            recv_sem=grecv_sem.at[way],
            device_id=peer(way),
            device_id_type=MESH,
        )

    def relay(way):
        gain_copy(way).wait_recv()
        gout[way] = (gmine[...] + gin[way].astype(f32)).astype(bf16)
        gain_copy(way).start()

    for way, goes, comes in ways:
        @pl.when(goes & jnp.logical_not(comes))
        def _():
            gout[way] = gmine[...].astype(bf16)
            gain_copy(way).start()

    launch(half, CHUNKS - 1)

    @pl.loop(half + 1, n - 1)
    def _(j):
        @pl.loop(0, CHUNKS)
        def _(c):
            step(j, c)

    near = (me < half, me >= half)
    tile_n = 640 if width % 640 == 0 else HEAD_DIM
    tiles_n = width // tile_n

    def forward(c):
        @pl.loop(0, tiles_n)
        def _(i):
            ns = pl.ds(pl.multiple_of(i * tile_n, tile_n), tile_n)
            value = jnp.dot(held[:, cols(c)], w[cols(c), ns], preferred_element_type=f32)
            if c == 0:
                acc[:, ns] = value
            else:
                acc[:, ns] += value

    first, second = CHUNKS // 4, CHUNKS - 1
    for c in range(CHUNKS):
        arrive(n - 1, c)
        prepare(n - 1, c)
        if c == first:
            for way, goes, comes in ways:
                @pl.when(near[way] & goes & comes)
                def _():
                    relay(way)
        if c != second:
            launch(n - 1, c)
        take(n - 1, c)
        forward(c)
    for way, goes, comes in ways:
        @pl.when(near[1 - way] & goes & comes)
        def _():
            relay(way)
    launch(n - 1, second)

    for h in range(heads):
        hs = slice(h * HEAD_DIM, (h + 1) * HEAD_DIM)
        x = acc[:, hs] * scale_ref[...] + bias[:, hs]
        turned = x * cos[...] + pltpu.roll(x, HEAD_DIM // 2, 1) * sin[...]
        plain = lax.rem(me * heads + h, GROUP) == GROUP - 1
        qkv[:, hs] = jnp.where(plain, x, turned).astype(bf16)

    loads[5].wait()
    scale = scale_ref[block(me), :][:, :1]
    inner = jnp.zeros((rows, 1), f32)
    for c in range(CHUNKS):
        ks = slice(c * span, (c + 1) * span)
        if c == CHUNKS - 1:
            for way, goes, comes in ways:
                @pl.when(comes & jnp.logical_not(goes))
                def _():
                    gain_copy(way).wait_recv()

                @pl.when(comes)
                def _():
                    gmine[...] += gin[way].astype(f32)
            for i in range(16):
                gg_ref[:, i * piece:(i + 1) * piece] = gmine[i:i + 1, :]
        tgp[:, ks] = part[block(me), ks]
        for way, goes, comes in ways:
            @pl.when(comes)
            def _():
                slot = me + 1 - way
                transfer(way, run, slot, n - 1, c).wait_recv()
                tgp[:, ks] += run[block(slot), ks].astype(f32)

        scaled = tgp[:, ks] * gain[:, ks]
        inner = inner + jnp.sum(scaled * tok[:, ks].astype(f32), axis=1, keepdims=True)
        tgp[:, ks] = scaled * scale

    weight[...] = jnp.broadcast_to(scale * scale * scale * (inner / depth), weight.shape)

    @pl.loop(0, n)
    def _(j):
        @pl.loop(0, CHUNKS)
        def _(c):
            for way, goes, comes in ways:
                @pl.when(goes)
                def _():
                    transfer(way, raw, 0, j, c).wait_send()

    for way, goes, comes in ways:
        @pl.when(goes)
        def _():
            gain_copy(way).wait_send()


def finish(qkv, tgp, tok, weight, gg, bg, qkv_h, tg_h, gg_h, bg_h, tg, sem):
    moves = ((qkv, qkv_h), (gg.at[0], gg_h), (bg.at[0], bg_h))
    copies = [pltpu.make_async_copy(src, dst, sem.at[i]) for i, (src, dst) in enumerate(moves)]
    for c in copies:
        c.start()
    factor = weight[:, :1]
    span = tg.shape[1] // PIECES
    for p in range(PIECES):
        ks = slice(p * span, (p + 1) * span)
        tg[:, ks] = tgp[:, ks] - tok[:, ks].astype(jnp.float32) * factor
        c = pltpu.make_async_copy(tg.at[:, ks], tg_h.at[:, ks], sem.at[3 + p])
        c.start()
        copies.append(c)
    for c in copies:
        c.wait()


def shards(n, tokens, norm_gain, qkv_weight, qkv_bias, qkv_grad):
    rows, depth = tokens.shape
    every, width = qkv_grad.shape
    cosine, sine = rope_tables(every, rows, SEQ_LEN // n)
    bf16, f32 = jnp.bfloat16, jnp.float32
    dma = pltpu.SemaphoreType.DMA
    hbm = pl.BlockSpec(memory_space=pl.ANY)
    vmem = pl.BlockSpec(memory_space=pltpu.VMEM)
    results = pl.pallas_call(
        functools.partial(kernel, n),
        out_shape=(
            pltpu.VMEM((every, width), bf16),
            pltpu.VMEM((rows, depth), f32),
            pltpu.VMEM((rows, depth), bf16),
            pltpu.VMEM((rows, HEAD_DIM), f32),
            pltpu.VMEM((1, depth), f32),
            pltpu.VMEM((1, width), f32),
        ),
        in_specs=[hbm] * 7,
        out_specs=[vmem] * 6,
        scratch_shapes=[
            pltpu.VMEM((every, depth), bf16),
            pltpu.VMEM((1, depth), f32),
            pltpu.VMEM((depth, width), bf16),
            pltpu.VMEM((1, width), f32),
            pltpu.VMEM((every, width), bf16),
            pltpu.VMEM((every, HEAD_DIM), f32),
            pltpu.VMEM((every, HEAD_DIM), f32),
            pltpu.VMEM((every, width), bf16),
            pltpu.VMEM((every, depth), f32),
            pltpu.VMEM((every, depth), bf16),
            pltpu.VMEM((every + rows, depth), bf16),
            pltpu.VMEM((every, width), f32),
            pltpu.VMEM((every, HEAD_DIM), f32),
            pltpu.VMEM((every, HEAD_DIM), f32),
            pltpu.VMEM((8, depth), f32),
            pltpu.VMEM((16, depth // 16), f32),
            pltpu.VMEM((2, 16, depth // 16), bf16),
            pltpu.VMEM((2, 16, depth // 16), bf16),
            dma((CHUNKS,)),
            dma((6,)),
            dma((depth // TILE_K,)),
            dma((2, n, CHUNKS)),
            dma((2, n, CHUNKS)),
            dma((2,)),
            dma((2,)),
            pltpu.SemaphoreType.REGULAR,
        ],
        compiler_params=pltpu.CompilerParams(
            collective_id=0, has_side_effects=True, vmem_limit_bytes=60000000
        ),
        cost_estimate=pl.CostEstimate(
            flops=4 * every * depth * width, bytes_accessed=2 * depth * width, transcendentals=0
        ),
    )(
        tokens, norm_gain, qkv_weight, qkv_bias, qkv_grad,
        jnp.asarray(cosine), jnp.asarray(sine),
    )
    return pl.pallas_call(
        finish,
        out_shape=(
            jax.ShapeDtypeStruct((every, width), bf16),
            jax.ShapeDtypeStruct((rows, depth), f32),
            jax.ShapeDtypeStruct((depth,), f32),
            jax.ShapeDtypeStruct((width,), f32),
        ),
        in_specs=[vmem] * 6,
        out_specs=[hbm] * 4,
        scratch_shapes=[pltpu.VMEM((rows, depth), f32), dma((3 + PIECES,))],
        compiler_params=pltpu.CompilerParams(vmem_limit_bytes=3 << 20),
    )(*results)


def solution(mesh):
    in_specs = (P(("dp", "mp"), None), P(), P(None, "mp"), P("mp"), P("dp", "mp"))
    out_specs = (P("dp", "mp"), P(("dp", "mp"), None), P("dp"), P(("dp", "mp")))
    body = functools.partial(shards, mesh.shape["mp"])
    return jax.shard_map(body, mesh=mesh, in_specs=in_specs, out_specs=out_specs, check_vma=False)
```

time: 54.9 us -> 54.4 us (level)
  no operation moved by 1% of the time
where the time goes in v1:
time: 54.4 us; the launch traced here: 54.3 us
  Pallas kernels  53.6 us (99%)
  between operations  0.64 us (1%)
    pallas_call x1, Pallas kernels, shards(): pl.pallas_call(functools.partial(kernel, n), out_shape=(pltpu.VMEM((every...  52.4 us
    pallas_call x1, Pallas kernels, shards(): pl.pallas_call(finish, out_shape=(jax.ShapeDtypeStruct((every, width), bf...  1.26 us

profile of v1, /device:TPU:0, one launch (start us, length us, event | category | flops | bytes accessed | tf_op | source)
XLA Modules:
  0.0 54.3 jit_solution(5952979068636560641)
XLA Ops:
  0.6 52.4 %shard_map.102 = (bf16[128,2560]{1,0:T(8,128)(2,1)S(1)}, f32[32,8192]{1,0:T(8,128)S(1)}, bf16[32,8192]{1,0:T(8,128)(2,1)S(1)}, f32[32,128]{1,0:T(8,128)S(1)}, f3...) custom-call(bf16[32,8192]{1,0:T(8,128)(2,1)} %tok_h.1, f32[8192]{0:T(1024)} %gain_h.1, bf16[8192,2560]{1,0:T(8,128)(2,1)} %w_h.1, ...), custom_call_target="tpu_custom_call" | custom-call | flops 10737418240 | bytes 41943040 | tf_op jit(solution)/shard_map/pallas_call | solution.py:412
  53.0 1.3 %shard_map.103 = (bf16[128,2560]{1,0:T(8,128)(2,1)}, f32[32,8192]{1,0:T(8,128)}, f32[8192]{0:T(1024)}, f32[2560]{0:T(1024)}) custom-call(bf16[128,2560]{1,0:T(8,128)(2,1)S(1)} %get-tuple-element.10.qkv, f32[32,8192]{1,0:T(8,128)S(1)} %get-tuple-element.11.tgp, bf16[32,8192]{1,0:T(8,128)(2,1)S(1)} %get-tuple-element.12.tok, ...), custom_call_target="tpu_custom_call" | custom-call | tf_op jit(solution)/shard_map/pallas_call | solution.py:462

commit v2 on v1

--- a/solution.py
+++ b/solution.py
@@ -14,6 +14,7 @@
 CHUNKS = 4
 TILE_K = 512
 PIECES = 4
+DEPTH = 4
 MESH = pl.DeviceIdType.MESH
 
 
@@ -32,22 +33,26 @@
 
 def kernel(
     n,
-    tok_h, gain_h, w_h, bias_h, grad_h, cos_h, sin_h,
+    tok_h, gain_h, w_h, bias_h, grad_h, turn_h,
     qkv, tgp, tok, weight, gg_ref, bg_ref,
-    raw, gain, w, bias, grad, cos, sin,
+    raw, gain, w, bias, grad, turn,
     low, part, held, run, acc, square, scale_ref, gsum, gmine, gout, gin,
-    tok_sem, in_sem, w_sem, send_sem, recv_sem, gsend_sem, grecv_sem, ready,
+    in_sem, w_sem, send_sem, recv_sem, gsend_sem, grecv_sem, ready,
 ):
     me = lax.axis_index("mp")
     rows, depth = tok.shape
     width = w.shape[1]
     heads = width // HEAD_DIM
+    fold = 4 if heads % 4 == 0 else 1
     span = depth // CHUNKS
     tiles = depth // TILE_K
     per = tiles // CHUNKS
     half = n // 2
     f32, bf16 = jnp.float32, jnp.bfloat16
-
+    every = low.shape[0]
+    cos, sin = turn.at[:every], turn.at[every:]
+
+    patient = lax.rem(lax.axis_index("dp"), 2) == 1
     has_right, has_left = me < n - 1, me > 0
     ways = ((0, has_right, has_left), (1, has_left, has_right))
     barrier = pltpu.get_barrier_semaphore()
@@ -65,31 +70,34 @@
     def cols(c):
         return pl.ds(pl.multiple_of(c * span, span), span)
 
-    def tok_copy(c):
-        return pltpu.make_async_copy(
-            tok_h.at[:, cols(c)], raw.at[block(me), cols(c)], tok_sem.at[c]
-        )
-
-    for c in range(CHUNKS):
-        tok_copy(c).start()
     loads = []
-    for i, (src, dst) in enumerate(
-        ((gain_h, gain.at[0]), (grad_h, grad), (cos_h, cos), (sin_h, sin), (bias_h, bias.at[0]), (tok_h, tok))
-    ):
+    for i, (src, dst) in enumerate((
+        (tok_h, raw.at[block(me), :]), (gain_h, gain.at[0]), (grad_h, grad),
+        (turn_h, turn), (bias_h, bias.at[0]),
+    )):
         loads.append(pltpu.make_async_copy(src, dst, in_sem.at[i]))
-        loads[i].start()
 
     def w_copy(i):
         k = pl.ds(pl.multiple_of(i * TILE_K, TILE_K), TILE_K)
-        return pltpu.make_async_copy(w_h.at[k, :], w.at[k, :], w_sem.at[i])
+        return pltpu.make_async_copy(w_h.at[k, :], w.at[k, :], w_sem.at[lax.rem(i, DEPTH)])
 
     def transfer(way, buf, at, j, c):
         ref = buf.at[block(at), cols(c)]
         return pltpu.make_async_remote_copy(
             src_ref=ref,
             dst_ref=ref,
-            send_sem=send_sem.at[way, j, c],
-            recv_sem=recv_sem.at[way, j, c],
+            send_sem=send_sem.at[way, c],
+            recv_sem=recv_sem.at[way, lax.rem(j, 2), c],
+            device_id=peer(way),
+            device_id_type=MESH,
+        )
+
+    def own(way, c):
+        return pltpu.make_async_remote_copy(
+            src_ref=tok_h.at[:, cols(c)],
+            dst_ref=raw.at[block(me), cols(c)],
+            send_sem=send_sem.at[way, c],
+            recv_sem=recv_sem.at[way, 0, c],
             device_id=peer(way),
             device_id_type=MESH,
         )
@@ -111,27 +119,29 @@
         total = jnp.sum(square[block(b), :], axis=1, keepdims=True)
         scale_ref[block(b), :] = jnp.broadcast_to(lax.rsqrt(total / depth + 1e-06), (rows, HEAD_DIM))
 
+    def send(way):
+        for c in range(CHUNKS):
+            own(way, c).start()
+
     @pl.when(has_left)
     def _():
         pl.semaphore_wait(barrier, 1)
         pl.semaphore_signal(ready, inc=1, device_id=peer(1), device_id_type=MESH)
-
-    for c in range(CHUNKS):
-        tok_copy(c).wait()
-
-        @pl.when(has_left)
-        def _():
-            transfer(1, raw, me, 0, c).start()
-
-    @pl.loop(0, tiles)
+        send(1)
+
+    for l in loads:
+        l.start()
+
+    @pl.loop(0, DEPTH)
     def _(i):
         w_copy(i).start()
+
+    loads[0].wait()
 
     @pl.when(has_right)
     def _():
         pl.semaphore_wait(ready, 1)
-        for c in range(CHUNKS):
-            transfer(0, raw, me, 0, c).start()
+        send(0)
 
     def arrive(j, c):
         for way, goes, comes in ways:
@@ -160,6 +170,10 @@
     def launch(j, c):
         for way, goes, comes in ways:
             back = me if way == 0 else n - 1 - me
+
+            @pl.when(goes)
+            def _():
+                transfer(way, raw, 0, 0, c).wait_send()
 
             @pl.when(goes & (j <= back))
             def _():
@@ -192,22 +206,31 @@
         launch(j, c)
         take(j, c)
 
-    for l in loads[:5]:
+    for l in loads[1:5]:
         l.wait()
-    for h in range(heads):
-        hs = slice(h * HEAD_DIM, (h + 1) * HEAD_DIM)
-        x = grad[:, hs].astype(f32)
-        turned = x * cos[...] - pltpu.roll(x, HEAD_DIM // 2, 1) * sin[...]
-        plain = lax.rem(me * heads + h, GROUP) == GROUP - 1
-        x = jnp.where(plain, x, turned)
-        bg_ref[:, hs] = jnp.sum(x, axis=0, keepdims=True)
-        low[:, hs] = x.astype(bf16)
+
+    @pl.loop(0, heads // fold)
+    def _(i):
+        for p in range(fold):
+            h = i * fold + p
+            hs = pl.ds(pl.multiple_of(h * HEAD_DIM, HEAD_DIM), HEAD_DIM)
+            x = grad[:, hs].astype(f32)
+            turned = x * cos[...] - pltpu.roll(x, HEAD_DIM // 2, 1) * sin[...]
+            plain = lax.rem(me * heads + h, GROUP) == GROUP - 1
+            x = jnp.where(plain, x, turned)
+            bg_ref[:, hs] = jnp.sum(x, axis=0, keepdims=True)
+            low[:, hs] = x.astype(bf16)
 
     def backward(c):
         @pl.loop(0, per)
         def _(i):
             at = c * per + i
             w_copy(at).wait()
+
+            @pl.when(at + DEPTH < tiles)
+            def _():
+                w_copy(at + DEPTH).start()
+
             k = pl.ds(pl.multiple_of(at * TILE_K, TILE_K), TILE_K)
             part[:, k] = lax.dot_general(
                 low[...], w[k, :], (((1,), (1,)), ((), ())), preferred_element_type=f32
@@ -216,14 +239,14 @@
     @pl.loop(0, CHUNKS)
     def _(c):
         backward(c)
+        step(1, c)
+
+    @pl.loop(0, CHUNKS)
+    def _(c):
         absorb(me, c)
-
-        @pl.when(c > 0)
-        def _():
-            step(1, c - 1)
+        tok[:, cols(c)] = raw[block(me), cols(c)]
 
     settle(me)
-    step(1, CHUNKS - 1)
 
     @pl.loop(2, half)
     def _(j):
@@ -231,41 +254,47 @@
         def _(c):
             step(j, c)
 
-    for c in range(CHUNKS - 1):
-        step(half, c)
-    arrive(half, CHUNKS - 1)
-    prepare(half, CHUNKS - 1)
-    take(half, CHUNKS - 1)
-
-    def gain_add(t, slot):
-        source = part if slot is None else run
-        at = slice(t * rows, (t + 1) * rows) if slot is None else slice(slot * rows, (slot + 1) * rows)
-        scale = scale_ref[t * rows:(t + 1) * rows, :]
+    @pl.loop(0, CHUNKS)
+    def _(c):
+        arrive(half, c)
+        prepare(half, c)
+
+        @pl.when(c < CHUNKS - 1)
+        def _():
+            launch(half, c)
+
+        take(half, c)
+
+
+    def gain_add(source, at, t):
+        scale = scale_ref[block(t), :]
 
         @pl.loop(0, depth // 1024)
         def _(i):
             for p in range(1024 // HEAD_DIM):
                 k = pl.ds(pl.multiple_of(i * 1024 + p * HEAD_DIM, HEAD_DIM), HEAD_DIM)
-                x = source[at, k].astype(f32) * raw[t * rows:(t + 1) * rows, k].astype(f32) * scale
+                x = source[block(at), k].astype(f32) * raw[block(t), k].astype(f32) * scale
                 total = x[:8]
                 for r in range(8, rows, 8):
                     total = total + x[r:r + 8]
                 gsum[:, k] += total
 
     gsum[...] = jnp.zeros_like(gsum)
-    for t in range(n):
+
+    @pl.loop(0, n)
+    def _(t):
         @pl.when((me - t < half) & (t - me < half))
         def _():
-            gain_add(t, None)
-
-        if t + half < n:
-            @pl.when(me == t + half)
-            def _():
-                gain_add(t, t)
-        if t - half >= 0:
-            @pl.when(me == t - half)
-            def _():
-                gain_add(t, t + 1)
+            gain_add(part, t, t)
+
+    @pl.when(me >= half)
+    def _():
+        gain_add(run, me - half, me - half)
+
+    @pl.when(me + half < n)
+    def _():
+        gain_add(run, me + half + 1, me + half)
+
     piece = depth // 16
     for i in range(16):
         gmine[i:i + 1, :] = jnp.sum(gsum[:, i * piece:(i + 1) * piece], axis=0, keepdims=True)
@@ -308,42 +337,54 @@
         def _(i):
             ns = pl.ds(pl.multiple_of(i * tile_n, tile_n), tile_n)
             value = jnp.dot(held[:, cols(c)], w[cols(c), ns], preferred_element_type=f32)
-            if c == 0:
+
+            @pl.when(c == 0)
+            def _():
                 acc[:, ns] = value
-            else:
+
+            @pl.when(c > 0)
+            def _():
                 acc[:, ns] += value
 
     first, second = CHUNKS // 4, CHUNKS - 1
-    for c in range(CHUNKS):
+    @pl.loop(0, CHUNKS)
+    def _(c):
         arrive(n - 1, c)
         prepare(n - 1, c)
-        if c == first:
-            for way, goes, comes in ways:
-                @pl.when(near[way] & goes & comes)
-                def _():
-                    relay(way)
-        if c != second:
+        for way, goes, comes in ways:
+            @pl.when(
+                goes & comes & ((near[way] & (c == first)) | (near[1 - way] & (c == second)))
+            )
+            def _():
+                relay(way)
+
+        @pl.when(jnp.logical_not(patient & (c == CHUNKS - 1)))
+        def _():
             launch(n - 1, c)
+
         take(n - 1, c)
         forward(c)
-    for way, goes, comes in ways:
-        @pl.when(near[1 - way] & goes & comes)
-        def _():
-            relay(way)
-    launch(n - 1, second)
-
-    for h in range(heads):
-        hs = slice(h * HEAD_DIM, (h + 1) * HEAD_DIM)
-        x = acc[:, hs] * scale_ref[...] + bias[:, hs]
-        turned = x * cos[...] + pltpu.roll(x, HEAD_DIM // 2, 1) * sin[...]
-        plain = lax.rem(me * heads + h, GROUP) == GROUP - 1
-        qkv[:, hs] = jnp.where(plain, x, turned).astype(bf16)
-
-    loads[5].wait()
+
+    @pl.loop(0, heads // fold)
+    def _(i):
+        for p in range(fold):
+            h = i * fold + p
+            hs = pl.ds(pl.multiple_of(h * HEAD_DIM, HEAD_DIM), HEAD_DIM)
+            x = acc[:, hs] * scale_ref[...] + bias[:, hs]
+            turned = x * cos[...] + pltpu.roll(x, HEAD_DIM // 2, 1) * sin[...]
+            plain = lax.rem(me * heads + h, GROUP) == GROUP - 1
+            qkv[:, hs] = jnp.where(plain, x, turned).astype(bf16)
+
     scale = scale_ref[block(me), :][:, :1]
     inner = jnp.zeros((rows, 1), f32)
     for c in range(CHUNKS):
         ks = slice(c * span, (c + 1) * span)
+        if c == CHUNKS - 2:
+            @pl.when(patient)
+            def _():
+                pl.delay(1000)
+                launch(n - 1, CHUNKS - 1)
+
         if c == CHUNKS - 1:
             for way, goes, comes in ways:
                 @pl.when(comes & jnp.logical_not(goes))
@@ -369,19 +410,12 @@
 
     weight[...] = jnp.broadcast_to(scale * scale * scale * (inner / depth), weight.shape)
 
-    @pl.loop(0, n)
-    def _(j):
-        @pl.loop(0, CHUNKS)
-        def _(c):
-            for way, goes, comes in ways:
-                @pl.when(goes)
-                def _():
-                    transfer(way, raw, 0, j, c).wait_send()
-
     for way, goes, comes in ways:
         @pl.when(goes)
         def _():
             gain_copy(way).wait_send()
+            for c in range(CHUNKS):
+                transfer(way, raw, 0, 0, c).wait_send()
 
 
 def finish(qkv, tgp, tok, weight, gg, bg, qkv_h, tg_h, gg_h, bg_h, tg, sem):
@@ -419,7 +453,7 @@
             pltpu.VMEM((1, depth), f32),
             pltpu.VMEM((1, width), f32),
         ),
-        in_specs=[hbm] * 7,
+        in_specs=[hbm] * 6,
         out_specs=[vmem] * 6,
         scratch_shapes=[
             pltpu.VMEM((every, depth), bf16),
@@ -427,8 +461,7 @@
             pltpu.VMEM((depth, width), bf16),
             pltpu.VMEM((1, width), f32),
             pltpu.VMEM((every, width), bf16),
-            pltpu.VMEM((every, HEAD_DIM), f32),
-            pltpu.VMEM((every, HEAD_DIM), f32),
+            pltpu.VMEM((2 * every, HEAD_DIM), f32),
             pltpu.VMEM((every, width), bf16),
             pltpu.VMEM((every, depth), f32),
             pltpu.VMEM((every, depth), bf16),
@@ -440,11 +473,10 @@
             pltpu.VMEM((16, depth // 16), f32),
             pltpu.VMEM((2, 16, depth // 16), bf16),
             pltpu.VMEM((2, 16, depth // 16), bf16),
-            dma((CHUNKS,)),
-            dma((6,)),
-            dma((depth // TILE_K,)),
-            dma((2, n, CHUNKS)),
-            dma((2, n, CHUNKS)),
+            dma((5,)),
+            dma((DEPTH,)),
+            dma((2, CHUNKS)),
+            dma((2, 2, CHUNKS)),
             dma((2,)),
             dma((2,)),
             pltpu.SemaphoreType.REGULAR,
@@ -457,7 +489,7 @@
         ),
     )(
         tokens, norm_gain, qkv_weight, qkv_bias, qkv_grad,
-        jnp.asarray(cosine), jnp.asarray(sine),
+        jnp.asarray(np.concatenate([cosine, sine])),
     )
     return pl.pallas_call(
         finish,

time: 54.4 us -> 51.3 us (0.943)
  Pallas kernels: 53.6 us -> 50.5 us
    pallas_call x1, Pallas kernels: 52.4 us -> 49.3 us  [shards(): pl.pallas_call(functools.partial(kernel, n), out_shape=(pltpu.VMEM((every...]
where the time goes in v2:
time: 51.3 us; the launch traced here: 51.2 us
  Pallas kernels  50.5 us (98%)
  between operations  0.64 us (1%)
    pallas_call x1, Pallas kernels, shards(): pl.pallas_call(functools.partial(kernel, n), out_shape=(pltpu.VMEM((every...  49.3 us
    pallas_call x1, Pallas kernels, shards(): pl.pallas_call(finish, out_shape=(jax.ShapeDtypeStruct((every, width), bf...  1.26 us

profile of v2, /device:TPU:0, one launch (start us, length us, event | category | flops | bytes accessed | tf_op | source)
XLA Modules:
  0.0 51.2 jit_solution(14937025572788063080)
XLA Ops:
  0.6 49.3 %shard_map.93 = (bf16[128,2560]{1,0:T(8,128)(2,1)S(1)}, f32[32,8192]{1,0:T(8,128)S(1)}, bf16[32,8192]{1,0:T(8,128)(2,1)S(1)}, f32[32,128]{1,0:T(8,128)S(1)}, f32...) custom-call(bf16[32,8192]{1,0:T(8,128)(2,1)} %tok_h.1, f32[8192]{0:T(1024)} %gain_h.1, bf16[8192,2560]{1,0:T(8,128)(2,1)} %w_h.1, ...), custom_call_target="tpu_custom_call" | custom-call | flops 10737418240 | bytes 41943040 | tf_op jit(solution)/shard_map/pallas_call | solution.py:446
  49.9 1.3 %shard_map.94 = (bf16[128,2560]{1,0:T(8,128)(2,1)}, f32[32,8192]{1,0:T(8,128)}, f32[8192]{0:T(1024)}, f32[2560]{0:T(1024)}) custom-call(bf16[128,2560]{1,0:T(8,128)(2,1)S(1)} %get-tuple-element.10.qkv, f32[32,8192]{1,0:T(8,128)S(1)} %get-tuple-element.11.tgp, bf16[32,8192]{1,0:T(8,128)(2,1)S(1)} %get-tuple-element.12.tok, ...), custom_call_target="tpu_custom_call" | custom-call | tf_op jit(solution)/shard_map/pallas_call | solution.py:494

commit v3 on v2

--- a/solution.py
+++ b/solution.py
@@ -13,7 +13,8 @@
 GROUP = 10
 CHUNKS = 4
 TILE_K = 512
-PIECES = 4
+PIECES = 2
+DELAY = 1600
 DEPTH = 4
 MESH = pl.DeviceIdType.MESH
 
@@ -36,7 +37,7 @@
     tok_h, gain_h, w_h, bias_h, grad_h, turn_h,
     qkv, tgp, tok, weight, gg_ref, bg_ref,
     raw, gain, w, bias, grad, turn,
-    low, part, held, run, acc, square, scale_ref, gsum, gmine, gout, gin,
+    low, part, held, run, acc, square, scale_ref, gsum, gmine, gout, gin, sums,
     in_sem, w_sem, send_sem, recv_sem, gsend_sem, grecv_sem, ready,
 ):
     me = lax.axis_index("mp")
@@ -86,29 +87,43 @@
         return pltpu.make_async_remote_copy(
             src_ref=ref,
             dst_ref=ref,
-            send_sem=send_sem.at[way, c],
+            send_sem=send_sem.at[way, lax.rem(j, 2)],
             recv_sem=recv_sem.at[way, lax.rem(j, 2), c],
             device_id=peer(way),
             device_id_type=MESH,
         )
 
+    def drain(way, j):
+        ref = raw.at[block(0), :]
+        pltpu.make_async_remote_copy(
+            src_ref=ref,
+            dst_ref=ref,
+            send_sem=send_sem.at[way, lax.rem(j, 2)],
+            recv_sem=recv_sem.at[way, 0, 0],
+            device_id=peer(way),
+            device_id_type=MESH,
+        ).wait_send()
+
     def own(way, c):
         return pltpu.make_async_remote_copy(
             src_ref=tok_h.at[:, cols(c)],
             dst_ref=raw.at[block(me), cols(c)],
-            send_sem=send_sem.at[way, c],
+            send_sem=send_sem.at[way, 0],
             recv_sem=recv_sem.at[way, 0, c],
             device_id=peer(way),
             device_id_type=MESH,
         )
 
+    def lanes(v):
+        while v.shape[1] > HEAD_DIM:
+            m = v.shape[1] // 2
+            v = v[:, :m] + v[:, m:]
+        return v
+
     def absorb(b, c):
         v = raw[block(b), cols(c)].astype(f32)
         held[block(b), cols(c)] = (v * gain[:, cols(c)]).astype(bf16)
-        v = v * v
-        while v.shape[1] > HEAD_DIM:
-            m = v.shape[1] // 2
-            v = v[:, :m] + v[:, m:]
+        v = lanes(v * v)
         if isinstance(c, int):
             old = jnp.zeros_like(v) if c == 0 else square[block(b), :]
         else:
@@ -171,9 +186,10 @@
         for way, goes, comes in ways:
             back = me if way == 0 else n - 1 - me
 
-            @pl.when(goes)
-            def _():
-                transfer(way, raw, 0, 0, c).wait_send()
+            if not isinstance(j, int) or j >= 2:
+                @pl.when(goes & (c == 0))
+                def _():
+                    drain(way, j)
 
             @pl.when(goes & (j <= back))
             def _():
@@ -376,13 +392,22 @@
             qkv[:, hs] = jnp.where(plain, x, turned).astype(bf16)
 
     scale = scale_ref[block(me), :][:, :1]
-    inner = jnp.zeros((rows, 1), f32)
+    sums[...] = jnp.zeros_like(sums)
+
+    def close(ks, slots):
+        value = part[block(me), ks]
+        for slot in slots:
+            value = value + run[block(slot), ks].astype(f32)
+        value = value * gain[:, ks]
+        tgp[:, ks] = value * scale
+        sums[...] += lanes(value * tok[:, ks].astype(f32))
+
     for c in range(CHUNKS):
         ks = slice(c * span, (c + 1) * span)
         if c == CHUNKS - 2:
             @pl.when(patient)
             def _():
-                pl.delay(1000)
+                pl.delay(DELAY)
                 launch(n - 1, CHUNKS - 1)
 
         if c == CHUNKS - 1:
@@ -396,26 +421,32 @@
                     gmine[...] += gin[way].astype(f32)
             for i in range(16):
                 gg_ref[:, i * piece:(i + 1) * piece] = gmine[i:i + 1, :]
-        tgp[:, ks] = part[block(me), ks]
         for way, goes, comes in ways:
             @pl.when(comes)
             def _():
-                slot = me + 1 - way
-                transfer(way, run, slot, n - 1, c).wait_recv()
-                tgp[:, ks] += run[block(slot), ks].astype(f32)
-
-        scaled = tgp[:, ks] * gain[:, ks]
-        inner = inner + jnp.sum(scaled * tok[:, ks].astype(f32), axis=1, keepdims=True)
-        tgp[:, ks] = scaled * scale
-
+                transfer(way, run, me + 1 - way, n - 1, c).wait_recv()
+
+        @pl.when(has_left & has_right)
+        def _():
+            close(ks, (me + 1, me))
+
+        @pl.when(jnp.logical_not(has_right))
+        def _():
+            close(ks, (me + 1,))
+
+        @pl.when(jnp.logical_not(has_left))
+        def _():
+            close(ks, (me,))
+
+    inner = jnp.sum(sums[...], axis=1, keepdims=True)
     weight[...] = jnp.broadcast_to(scale * scale * scale * (inner / depth), weight.shape)
 
     for way, goes, comes in ways:
         @pl.when(goes)
         def _():
             gain_copy(way).wait_send()
-            for c in range(CHUNKS):
-                transfer(way, raw, 0, 0, c).wait_send()
+            drain(way, n - 2)
+            drain(way, n - 1)
 
 
 def finish(qkv, tgp, tok, weight, gg, bg, qkv_h, tg_h, gg_h, bg_h, tg, sem):
@@ -473,9 +504,10 @@
             pltpu.VMEM((16, depth // 16), f32),
             pltpu.VMEM((2, 16, depth // 16), bf16),
             pltpu.VMEM((2, 16, depth // 16), bf16),
+            pltpu.VMEM((rows, HEAD_DIM), f32),
             dma((5,)),
             dma((DEPTH,)),
-            dma((2, CHUNKS)),
+            dma((2, 2)),
             dma((2, 2, CHUNKS)),
             dma((2,)),
             dma((2,)),

time: 51.3 us -> 51.2 us (level)
  no operation moved by 1% of the time
where the time goes in v3:
time: 51.2 us; the launch traced here: 50.7 us
  Pallas kernels  50.1 us (98%)
  between operations  0.64 us (1%)
    pallas_call x1, Pallas kernels, shards(): pl.pallas_call(functools.partial(kernel, n), out_shape=(pltpu.VMEM((every...  48.9 us
    pallas_call x1, Pallas kernels, shards(): pl.pallas_call(finish, out_shape=(jax.ShapeDtypeStruct((every, width), bf...  1.24 us

profile of v3, /device:TPU:0, one launch (start us, length us, event | category | flops | bytes accessed | tf_op | source)
XLA Modules:
  0.0 50.7 jit_solution(3225218981464754349)
XLA Ops:
  0.6 48.9 %shard_map.93 = (bf16[128,2560]{1,0:T(8,128)(2,1)S(1)}, f32[32,8192]{1,0:T(8,128)S(1)}, bf16[32,8192]{1,0:T(8,128)(2,1)S(1)}, f32[32,128]{1,0:T(8,128)S(1)}, f32...) custom-call(bf16[32,8192]{1,0:T(8,128)(2,1)} %tok_h.1, f32[8192]{0:T(1024)} %gain_h.1, bf16[8192,2560]{1,0:T(8,128)(2,1)} %w_h.1, ...), custom_call_target="tpu_custom_call" | custom-call | flops 10737418240 | bytes 41943040 | tf_op jit(solution)/shard_map/pallas_call | solution.py:477
  49.5 1.2 %shard_map.94 = (bf16[128,2560]{1,0:T(8,128)(2,1)}, f32[32,8192]{1,0:T(8,128)}, f32[8192]{0:T(1024)}, f32[2560]{0:T(1024)}) custom-call(bf16[128,2560]{1,0:T(8,128)(2,1)S(1)} %get-tuple-element.10.qkv, f32[32,8192]{1,0:T(8,128)S(1)} %get-tuple-element.11.tgp, bf16[32,8192]{1,0:T(8,128)(2,1)S(1)} %get-tuple-element.12.tok, ...), custom_call_target="tpu_custom_call" | custom-call | tf_op jit(solution)/shard_map/pallas_call | solution.py:526

commit v4 on v2

--- a/solution.py
+++ b/solution.py
@@ -13,7 +13,7 @@
 GROUP = 10
 CHUNKS = 4
 TILE_K = 512
-PIECES = 4
+PIECES = 2
 DEPTH = 4
 MESH = pl.DeviceIdType.MESH
 
@@ -382,7 +382,7 @@
         if c == CHUNKS - 2:
             @pl.when(patient)
             def _():
-                pl.delay(1000)
+                pl.delay(1600)
                 launch(n - 1, CHUNKS - 1)
 
         if c == CHUNKS - 1:

time: 51.3 us -> 51.2 us (level)
  no operation moved by 1% of the time
where the time goes in v4:
time: 51.2 us; the launch traced here: 50.8 us
  Pallas kernels  50.1 us (98%)
  between operations  0.64 us (1%)
    pallas_call x1, Pallas kernels, shards(): pl.pallas_call(functools.partial(kernel, n), out_shape=(pltpu.VMEM((every...  48.9 us
    pallas_call x1, Pallas kernels, shards(): pl.pallas_call(finish, out_shape=(jax.ShapeDtypeStruct((every, width), bf...  1.24 us

profile of v4, /device:TPU:0, one launch (start us, length us, event | category | flops | bytes accessed | tf_op | source)
XLA Modules:
  0.0 50.8 jit_solution(3183140168590995718)
XLA Ops:
  0.6 48.9 %shard_map.93 = (bf16[128,2560]{1,0:T(8,128)(2,1)S(1)}, f32[32,8192]{1,0:T(8,128)S(1)}, bf16[32,8192]{1,0:T(8,128)(2,1)S(1)}, f32[32,128]{1,0:T(8,128)S(1)}, f32...) custom-call(bf16[32,8192]{1,0:T(8,128)(2,1)} %tok_h.1, f32[8192]{0:T(1024)} %gain_h.1, bf16[8192,2560]{1,0:T(8,128)(2,1)} %w_h.1, ...), custom_call_target="tpu_custom_call" | custom-call | flops 10737418240 | bytes 41943040 | tf_op jit(solution)/shard_map/pallas_call | solution.py:446
  49.5 1.2 %shard_map.94 = (bf16[128,2560]{1,0:T(8,128)(2,1)}, f32[32,8192]{1,0:T(8,128)}, f32[8192]{0:T(1024)}, f32[2560]{0:T(1024)}) custom-call(bf16[128,2560]{1,0:T(8,128)(2,1)S(1)} %get-tuple-element.10.qkv, f32[32,8192]{1,0:T(8,128)S(1)} %get-tuple-element.11.tgp, bf16[32,8192]{1,0:T(8,128)(2,1)S(1)} %get-tuple-element.12.tok, ...), custom_call_target="tpu_custom_call" | custom-call | tf_op jit(solution)/shard_map/pallas_call | solution.py:494
